TPU v7x, 32 devices: a whole 2x2x4 slice. The times are simulated.
32 devices in a mesh: row: 4 (over y, x), col: 4 (over z), crop: 2 (over core).
Axes of the slice: x: 2, y: 2, z: 4, core: 2. Of those that a mesh axis runs over, the one named last changes fastest.
Arguments:
- pair_repr: bfloat16 [256, 128, 128], P(('crop', 'row'), 'col'), parts along dimension 0, may hold values from -6 to 6
- pair_mask: int32 [256, 128], P(('crop', 'row'), 'col'), parts along dimension 0, may hold values 0 or 1
- out_left_w: bfloat16 [128, 256], replicated, may hold values from -0.5 to 0.5
- out_right_w: bfloat16 [128, 256], replicated, may hold values from -0.5 to 0.5
- out_gate_w: bfloat16 [128, 128], replicated, may hold values from -0.5 to 0.5
- out_final_w: bfloat16 [128, 128], replicated, may hold values from -0.5 to 0.5
- in_left_w: bfloat16 [128, 256], replicated, may hold values from -0.5 to 0.5
- in_right_w: bfloat16 [128, 256], replicated, may hold values from -0.5 to 0.5
- in_gate_w: bfloat16 [128, 128], replicated, may hold values from -0.5 to 0.5
- in_final_w: bfloat16 [128, 128], replicated, may hold values from -0.5 to 0.5
- trans_in_w: bfloat16 [128, 1024], replicated, may hold values from -0.5 to 0.5
- trans_out_w: bfloat16 [512, 128], replicated, may hold values from -0.25 to 0.25
Outputs:
- pair_out: bfloat16 [256, 128, 128], P(('crop', 'row'), 'col'), parts along dimension 0
There are 2 independent parts, one for each index of `crop`. A program takes and returns all parts, laid end to end along the dimension named above; an argument that names none is the same for every part. Nothing has to cross between parts.
All inputs are finite; a program needn't handle non-finite values. No bound on the sum of `pair_mask` on one device may be relied on, other than what follows from the above.
Results may differ from a plain program's by a relative error of at most 0.015.
Values may be sent and summed in bfloat16 or wider, within the bound.
No kernel may reach another device: no remote copies, remote signals or barrier semaphores. Data moves between devices by JAX's collectives and lax.ppermute only.
A program may use at most 128 MiB of HBM per device.

v0:
```python
import jax
import jax.numpy as jnp
from jax import lax
from jax.sharding import PartitionSpec as P

epsilon = 1e-05


def layer_norm(values):
    average = jnp.mean(values, axis=-1, keepdims=True)
    centered = values - average
    spread = jnp.mean(centered * centered, axis=-1, keepdims=True)
    return centered * lax.rsqrt(spread + epsilon)


def gated(normed, weight, mask_vals):
    projected = jnp.dot(normed, weight, preferred_element_type=jnp.float32)
    half_width = weight.shape[1] // 2
    result = jax.nn.sigmoid(projected[..., :half_width]) * projected[..., half_width:]
    result = result * mask_vals[..., None]
    return result.astype(jnp.bfloat16)


def finish(pair_repr, normed, triangle, gate_w, final_w):
    gate_vals = jax.nn.sigmoid(jnp.dot(normed, gate_w, preferred_element_type=jnp.float32))
    tri_norm = layer_norm(triangle).astype(jnp.bfloat16)
    update = jnp.dot(tri_norm, final_w, preferred_element_type=jnp.float32)
    return (pair_repr.astype(jnp.float32) + gate_vals * update).astype(jnp.bfloat16)


def shards(
    pair_repr,
    pair_mask,
    out_left_w,
    out_right_w,
    out_gate_w,
    out_final_w,
    in_left_w,
    in_right_w,
    in_gate_w,
    in_final_w,
    trans_in_w,
    trans_out_w,
):
    mask_vals = pair_mask.astype(jnp.float32)
    normed_out = layer_norm(pair_repr.astype(jnp.float32)).astype(jnp.bfloat16)
    outbound = gated(normed_out, out_right_w, mask_vals)
    turned_right = lax.all_to_all(
        lax.all_to_all(outbound, "row", split_axis=0, concat_axis=0, tiled=True),
        "col",
        split_axis=0,
        concat_axis=1,
        tiled=True,
    )
    left_tile = gated(normed_out, out_left_w, mask_vals)
    gathered = lax.all_gather(left_tile, "col", axis=1, tiled=True)
    triangle = jnp.einsum(
        "ikh,jkh->ijh",
        gathered,
        lax.all_gather(turned_right, "row", axis=0, tiled=True),
        preferred_element_type=jnp.float32,
    )
    middle = finish(pair_repr, normed_out, triangle, out_gate_w, out_final_w)
    normed_in = layer_norm(middle.astype(jnp.float32)).astype(jnp.bfloat16)
    outbound_left = gated(normed_in, in_left_w, mask_vals)
    turned_left = lax.all_to_all(
        lax.all_to_all(outbound_left, "col", split_axis=1, concat_axis=1, tiled=True),
        "row",
        split_axis=1,
        concat_axis=0,
        tiled=True,
    )
    right_tile = gated(normed_in, in_right_w, mask_vals)
    column_panel = lax.all_gather(right_tile, "row", axis=0, tiled=True)
    triangle_in = jnp.einsum(
        "kih,kjh->ijh",
        lax.all_gather(turned_left, "col", axis=1, tiled=True),
        column_panel,
        preferred_element_type=jnp.float32,
    )
    after_in = finish(middle, normed_in, triangle_in, in_gate_w, in_final_w)
    normed_mix = layer_norm(after_in.astype(jnp.float32)).astype(jnp.bfloat16)
    projected = jnp.dot(normed_mix, trans_in_w, preferred_element_type=jnp.float32)
    half_width = trans_in_w.shape[1] // 2
    hidden = (jax.nn.silu(projected[..., :half_width]) * projected[..., half_width:]).astype(
        jnp.bfloat16
    )
    result = after_in.astype(jnp.float32) + jnp.dot(
        hidden, trans_out_w, preferred_element_type=jnp.float32
    )
    return result.astype(jnp.bfloat16)


def solution(mesh):
    in_specs = (
        P(("crop", "row"), "col", None),
        P(("crop", "row"), "col"),
        P(),
        P(),
        P(),
        P(),
        P(),
        P(),
        P(),
        P(),
        P(),
        P(),
    )
    out_specs = P(("crop", "row"), "col", None)
    return jax.shard_map(shards, mesh=mesh, in_specs=in_specs, out_specs=out_specs, check_vma=False)
```

profile of v0, /device:TPU:0, one launch (start us, length us, event | category | flops | bytes accessed | tf_op | source)
XLA Modules:
  0.0 162.0 jit_solution(13725264176336256992)
XLA Ops:
  6.5 1.2 convert_reduce_fusion
  7.8 1.3 fusion.17
  9.1 1.4 fusion.44
  10.6 1.3 fusion.46
  11.9 1.0 fusion.30
  13.0 10.7 %all_to_all.46 = bf16[32,32,128]{2,1,0:T(8,128)(2,1)S(1)} all-to-all(bf16[32,32,128]{2,1,0:T(8,128)(2,1)S(1)} %get-tuple-element.8), channel_id=1, replica_groups=mesh['row'=4,'col'=4,'crop'=2] {'row'}, dimensions={0} | all-to-all | bytes 524288 | tf_op jit(solution)/shard_map/all_to_all | solution.py:49
  23.7 21.0 %all_to_all.47 = bf16[32,32,128]{2,1,0:T(8,128)(2,1)S(1)} all-to-all(bf16[32,32,128]{2,1,0:T(8,128)(2,1)S(1)} %all_to_all.46), channel_id=1, replica_groups=mesh['row'=4,'col'=4,'crop'=2] {'col'}, dimensions={0} | all-to-all | bytes 524288 | tf_op jit(solution)/shard_map/all_to_all | solution.py:48
  44.7 0.9 copy.66
  45.7 0.7 fusion.6
  46.5 3.4 %all-gather.7.cloned.1.call-done = bf16[32,128,128]{2,1,0:T(8,128)(2,1)} async-done(((bf16[32,32,128]{2,1,0:T(8,128)(2,1)}), bf16[32,128,128]{2,1,0:T(8,128)(2,1)}) %all-gather.7.cloned.1.call-update) | async-done | bytes 1048592 | tf_op jit(solution)/shard_map/all_gather | solution.py:56
  49.9 2.7 %copy.67 = bf16[32,128,128]{1,0,2:T(8,128)(2,1)} copy(bf16[32,128,128]{2,1,0:T(8,128)(2,1)} %all-gather.7.cloned.1.call-done) | data formatting | bytes 2097152 | tf_op jit(solution)/shard_map/all_gather | solution.py:56
  52.5 24.4 %all-gather.5.cloned.1.call-done = bf16[32,128,128]{1,0,2:T(8,128)(2,1)} async-done(((bf16[8,128,128]{1,0,2:T(8,128)(2,1)}), bf16[32,128,128]{1,0,2:T(8,128)(2,1)}) %all-gather.5.cloned.1.call-update) | async-done | bytes 1048592 | tf_op jit(solution)/shard_map/all_gather | solution.py:60
  76.9 2.2 %bitcast_reduce_fusion.1 = (f32[32,32]{0,1:T(8,128)S(1)}, f32[128,32,32]{2,1,0:T(8,128)S(1)}) fusion(bf16[32,128,128]{1,0,2:T(8,128)(2,1)} %all-gather.5.cloned.1.call-done, bf16[32,128,128]{1,0,2:T(8,128)(2,1)} %copy.67), kind=kOutput, calls=%fused_computation.5 | convolution fusion | flops 33684480 | bytes 2625536 | tf_op jit(solution)/shard_map/ikh,jkh->ijh/dot_general | solution.py:57
  79.8 1.3 multiply_convert_fusion.1
  81.1 2.7 %copy.72 = bf16[32,32,128]{2,1,0:T(8,128)(2,1)S(1)} copy(bf16[32,32,128]{0,1,2:T(8,128)(2,1)} %multiply_convert_fusion.1) | data formatting | bytes 524288 | tf_op jit(solution)/shard_map/convert_element_type | solution.py:26
  83.8 0.4 fusion.60
  84.1 0.4 multiply_reduce_fusion.3
  85.5 1.0 fusion.20
  86.7 13.1 %all_to_all.48 = bf16[32,32,128]{2,0,1:T(8,128)(2,1)S(1)} all-to-all(bf16[32,32,128]{2,0,1:T(8,128)(2,1)S(1)} %copy.73), channel_id=1, replica_groups=mesh['row'=4,'col'=4,'crop'=2] {'col'}, dimensions={1} | all-to-all | bytes 524288 | tf_op jit(solution)/shard_map/all_to_all | solution.py:67
  99.8 8.2 %all_to_all.49 = bf16[32,32,128]{2,0,1:T(8,128)(2,1)S(1)} all-to-all(bf16[32,32,128]{2,0,1:T(8,128)(2,1)S(1)} %all_to_all.48), channel_id=1, replica_groups=mesh['row'=4,'col'=4,'crop'=2] {'row'}, dimensions={1} | all-to-all | bytes 524288 | tf_op jit(solution)/shard_map/all_to_all | solution.py:66
  108.1 0.9 copy.76
  109.1 1.1 fusion.3
  110.2 3.4 %all-gather.9.cloned.1.call-done = bf16[128,32,128]{2,1,0:T(8,128)(2,1)} async-done(((bf16[32,32,128]{2,1,0:T(8,128)(2,1)}), bf16[128,32,128]{2,1,0:T(8,128)(2,1)}) %all-gather.9.cloned.1.call-update) | async-done | bytes 1048592 | tf_op jit(solution)/shard_map/all_gather | solution.py:74
  113.6 3.2 %copy.77 = bf16[128,32,128]{0,1,2:T(8,128)(2,1)} copy(bf16[128,32,128]{2,1,0:T(8,128)(2,1)} %all-gather.9.cloned.1.call-done) | data formatting | bytes 2097152 | tf_op jit(solution)/shard_map/all_gather | solution.py:74
  116.8 27.7 %all-gather.11.cloned.1.call-done = bf16[128,32,128]{0,1,2:T(8,128)(2,1)} async-done(((bf16[128,8,128]{0,1,2:T(8,128)(2,1)}), bf16[128,32,128]{0,1,2:T(8,128)(2,1)}) %all-gather.11.cloned.1.call-update) | async-done | bytes 1048592 | tf_op jit(solution)/shard_map/all_gather | solution.py:77
  144.5 2.2 %bitcast_reduce_fusion = (f32[32,32]{0,1:T(8,128)S(1)}, f32[128,32,32]{2,1,0:T(8,128)S(1)}) fusion(bf16[128,32,128]{0,1,2:T(8,128)(2,1)} %copy.77, bf16[128,32,128]{0,1,2:T(8,128)(2,1)} %all-gather.11.cloned.1.call-done), kind=kOutput, calls=%fused_computation.3 | convolution fusion | flops 33684480 | bytes 2625536 | tf_op jit(solution)/shard_map/kih,kjh->ijh/dot_general | solution.py:75
  147.4 1.3 multiply_convert_fusion
  148.6 2.6 %copy.82 = bf16[32,32,128]{2,1,0:T(8,128)(2,1)S(1)} copy(bf16[32,32,128]{0,1,2:T(8,128)(2,1)} %multiply_convert_fusion) | data formatting | bytes 524288 | tf_op jit(solution)/shard_map/convert_element_type | solution.py:26
  151.3 1.4 fusion.61
  152.7 0.4 multiply_reduce_fusion.2
  153.1 0.8 fusion.39
  154.0 1.4 fusion.13
  (55 shorter events, 2.8 us)
Async XLA Ops:
  6.5 146.6 %copy-start = (bf16[128,1024]{1,0:T(8,128)(2,1)S(1)}, bf16[128,1024]{1,0:T(8,128)(2,1)}, u32[]{:S(2)}) copy-start(bf16[128,1024]{1,0:T(8,128)(2,1)} %param.22) | copy-start | bytes 786436
  6.5 4.0 %copy-start.1 = (bf16[32,32,128]{2,1,0:T(8,128)(2,1)S(1)}, bf16[32,32,128]{2,1,0:T(8,128)(2,1)}, u32[]{:S(2)}) copy-start(bf16[32,32,128]{2,1,0:T(8,128)(2,1)} %param.12) | copy-start | bytes 786436
  6.5 5.3 %copy-start.6 = (s32[32,32]{1,0:T(8,128)S(1)}, s32[32,32]{1,0:T(8,128)}, u32[]{:S(2)}) copy-start(s32[32,32]{1,0:T(8,128)} %param.13) | copy-start | bytes 12292
  6.5 43.3 %all-gather.7.cloned.1.call-start = ((), (), s32[]{:S(2)}) async-start(), calls=%async_computation.5 | async-start | bytes 1310720 | tf_op jit(solution)/shard_map/all_gather | solution.py:56
  11.9 33.8 %copy-start.8 = (bf16[128,128]{1,0:T(8,128)(2,1)S(1)}, bf16[128,128]{1,0:T(8,128)(2,1)}, u32[]{:S(2)}) copy-start(bf16[128,128]{1,0:T(8,128)(2,1)} %param.16) | copy-start | bytes 98308
  12.9 64.0 %all-gather.5.cloned.1.call-start = ((), (), s32[]{:S(2)}) async-start(), calls=%async_computation.4 | async-start | bytes 1310720 | tf_op jit(solution)/shard_map/all_gather | solution.py:60
  45.7 67.9 %all-gather.9.cloned.1.call-start = ((), (), s32[]{:S(2)}) async-start(), calls=%async_computation.6 | async-start | bytes 1310720 | tf_op jit(solution)/shard_map/all_gather | solution.py:74
  79.8 3.9 %copy-start.5 = (bf16[128,128]{1,0:T(8,128)(2,1)S(1)}, bf16[128,128]{1,0:T(8,128)(2,1)}, u32[]{:S(2)}) copy-start(bf16[128,128]{1,0:T(8,128)(2,1)} %param.17) | copy-start | bytes 98308
  81.1 3.8 %copy-start.2 = (bf16[128,256]{1,0:T(8,128)(2,1)S(1)}, bf16[128,256]{1,0:T(8,128)(2,1)}, u32[]{:S(2)}) copy-start(bf16[128,256]{1,0:T(8,128)(2,1)} %param.18) | copy-start | bytes 196612
  83.7 1.4 copy-start.3
  86.5 22.6 %copy-start.9 = (bf16[128,128]{1,0:T(8,128)(2,1)S(1)}, bf16[128,128]{1,0:T(8,128)(2,1)}, u32[]{:S(2)}) copy-start(bf16[128,128]{1,0:T(8,128)(2,1)} %param.20) | copy-start | bytes 98308
  86.5 58.0 %all-gather.11.cloned.1.call-start = ((), (), s32[]{:S(2)}) async-start(), calls=%async_computation.7 | async-start | bytes 1310720 | tf_op jit(solution)/shard_map/all_gather | solution.py:77
  147.4 3.9 %copy-start.4 = (bf16[128,128]{1,0:T(8,128)(2,1)S(1)}, bf16[128,128]{1,0:T(8,128)(2,1)}, u32[]{:S(2)}) copy-start(bf16[128,128]{1,0:T(8,128)(2,1)} %param.21) | copy-start | bytes 98308
  153.1 0.9 copy-start.7
Sparse Core Ops, SparseCore 0:
  13.1 36.7 all-gather.6
  51.7 25.2 all-gather.4
  86.6 26.9 all-gather.8
  115.0 29.4 all-gather.10
where the time goes:
time: 163 us; the launch traced here: 162 us
  waiting for transfers between devices  59 us (36%)
  blocking collectives  53.1 us (33%)
  local copies, waits for them, and re-layouts  14 us (9%)
  matrix products  13.4 us (8%)
  between operations  13.4 us (8%)
  other arithmetic  8.94 us (5%)
    all_gather x1, waiting for transfers between devices, shards(): lax.all_gather(turned_left, 'col', axis=1, tiled=True)  27.7 us
    all_gather x1, waiting for transfers between devices, shards(): lax.all_gather(turned_right, 'row', axis=0, tiled=True)  24.4 us
    all_to_all x1, blocking collectives, shards(): lax.all_to_all(lax.all_to_all(outbound, 'row', split_axis=0, concat_axis=...  21 us
    all_to_all x1, blocking collectives, shards(): lax.all_to_all(outbound_left, 'col', split_axis=1, concat_axis=1, tiled=T...  13.1 us
    all_to_all x1, blocking collectives, shards(): lax.all_to_all(outbound, 'row', split_axis=0, concat_axis=0, tiled=True)  10.7 us
    all_to_all x1, blocking collectives, shards(): lax.all_to_all(lax.all_to_all(outbound_left, 'col', split_axis=1, concat_...  8.25 us
    convert_element_type x2, local copies, waits for them, and re-layouts, finish(): tri_norm = layer_norm(triangle).astype(jnp.bfloat16)  5.27 us
    all_gather x1, waiting for transfers between devices, shards(): column_panel = lax.all_gather(right_tile, 'row', axis=0, tiled=True)  3.41 us
  transfers between devices with their start and end apart: 4, of which 4 were waited for; matrix products, arithmetic and copies ran while one was open for 6% of the time, Pallas kernels for 0%

commit v1 on v0

--- a/solution.py
+++ b/solution.py
@@ -54,12 +54,18 @@
     )
     left_tile = gated(normed_out, out_left_w, mask_vals)
     gathered = lax.all_gather(left_tile, "col", axis=1, tiled=True)
-    triangle = jnp.einsum(
-        "ikh,jkh->ijh",
-        gathered,
-        lax.all_gather(turned_right, "row", axis=0, tiled=True),
-        preferred_element_type=jnp.float32,
-    )
+    size, position, rows = (lax.axis_size("row"), lax.axis_index("row"), turned_right.shape[0])
+    forward = [(i, (i + 1) % size) for i in range(size)]
+    held, triangle = (turned_right, None)
+    for step in range(size):
+        holder = (position - step) % size
+        coming = lax.ppermute(held, "row", forward) if step < size - 1 else None
+        made = jnp.einsum("ikh,jkh->ijh", gathered, held, preferred_element_type=jnp.float32)
+        length = made.shape[1]
+        if triangle is None:
+            triangle = jnp.zeros((*made.shape[:1], size * length, *made.shape[1 + 1 :]), made.dtype)
+        triangle = lax.dynamic_update_slice_in_dim(triangle, made, holder * length, axis=1)
+        held = coming
     middle = finish(pair_repr, normed_out, triangle, out_gate_w, out_final_w)
     normed_in = layer_norm(middle.astype(jnp.float32)).astype(jnp.bfloat16)
     outbound_left = gated(normed_in, in_left_w, mask_vals)

time: 163 us -> 148 us (0.908)
  waiting for transfers between devices: 59 us -> 48.3 us
  local copies, waits for them, and re-layouts: 14 us -> 10.6 us
  blocking collectives: 53.1 us -> 50.7 us
  matrix products: 13.4 us -> 15.2 us
    all_gather x1 -> x0, waiting for transfers between devices: 24.4 us -> none  [shards(): lax.all_gather(turned_right, 'row', axis=0, tiled=True)]
    ppermute x0 -> x3, waiting for transfers between devices: none -> 16.1 us  [shards(): coming = lax.ppermute(held, 'row', forward) if step < size - 1 else None]
    all_gather x1, waiting for transfers between devices: 3.41 us -> 0.01 us  [shards(): gathered = lax.all_gather(left_tile, 'col', axis=1, tiled=True)]
    convert_element_type x2 -> x1, local copies, waits for them, and re-layouts: 5.27 us -> 2.62 us  [finish(): tri_norm = layer_norm(triangle).astype(jnp.bfloat16)]
    all_to_all x1, blocking collectives: 13.1 us -> 10.8 us  [shards(): lax.all_to_all(outbound_left, 'col', split_axis=1, concat_axis=1, tiled=T...]
    dot_general x1 -> x4, matrix products: 2.2 us -> 3.5 us  [shards(): jnp.einsum('ikh,jkh->ijh', gathered, held, preferred_element_type=jnp.flo...]
  transfers between devices with their start and end apart: 4 -> 6, of which waited for: 4 -> 5; matrix products, arithmetic and copies ran while one was open for 6% -> 7% of each run, Pallas kernels for 0% -> 0%
where the time goes in v1:
time: 148 us; the launch traced here: 147 us
  blocking collectives  50.7 us (34%)
  waiting for transfers between devices  48.3 us (33%)
  matrix products  15.2 us (10%)
  between operations  13.5 us (9%)
  local copies, waits for them, and re-layouts  10.6 us (7%)
  other arithmetic  7.93 us (5%)
    all_gather x1, waiting for transfers between devices, shards(): lax.all_gather(turned_left, 'col', axis=1, tiled=True)  28.3 us
    all_to_all x1, blocking collectives, shards(): lax.all_to_all(lax.all_to_all(outbound, 'row', split_axis=0, concat_axis=...  21 us
    ppermute x3, waiting for transfers between devices, shards(): coming = lax.ppermute(held, 'row', forward) if step < size - 1 else None  16.1 us
    all_to_all x1, blocking collectives, shards(): lax.all_to_all(outbound_left, 'col', split_axis=1, concat_axis=1, tiled=T...  10.8 us
    all_to_all x1, blocking collectives, shards(): lax.all_to_all(outbound, 'row', split_axis=0, concat_axis=0, tiled=True)  10.7 us
    all_to_all x1, blocking collectives, shards(): lax.all_to_all(lax.all_to_all(outbound_left, 'col', split_axis=1, concat_...  8.1 us
    all_gather x1, waiting for transfers between devices, shards(): column_panel = lax.all_gather(right_tile, 'row', axis=0, tiled=True)  3.85 us
    dot_general x4, matrix products, shards(): jnp.einsum('ikh,jkh->ijh', gathered, held, preferred_element_type=jnp.flo...  3.5 us
  transfers between devices with their start and end apart: 6, of which 5 were waited for; matrix products, arithmetic and copies ran while one was open for 7% of the time, Pallas kernels for 0%

profile of v1, /device:TPU:0, one launch (start us, length us, event | category | flops | bytes accessed | tf_op | source)
XLA Modules:
  0.0 147.3 jit_solution(13939790397222525213)
XLA Ops:
  6.5 1.2 convert_reduce_fusion
  7.8 1.3 fusion.17
  9.1 1.4 fusion.46
  10.6 1.3 fusion.48
  11.9 1.0 fusion.30
  13.0 10.7 %all_to_all.46 = bf16[32,32,128]{2,1,0:T(8,128)(2,1)S(1)} all-to-all(bf16[32,32,128]{2,1,0:T(8,128)(2,1)S(1)} %get-tuple-element.8), channel_id=1, replica_groups=mesh['row'=4,'col'=4,'crop'=2] {'row'}, dimensions={0} | all-to-all | bytes 524288 | tf_op jit(solution)/shard_map/all_to_all | solution.py:49
  23.7 21.0 %all_to_all.47 = bf16[32,32,128]{2,1,0:T(8,128)(2,1)S(1)} all-to-all(bf16[32,32,128]{2,1,0:T(8,128)(2,1)S(1)} %all_to_all.46), channel_id=1, replica_groups=mesh['row'=4,'col'=4,'crop'=2] {'col'}, dimensions={0} | all-to-all | bytes 524288 | tf_op jit(solution)/shard_map/all_to_all | solution.py:48
  44.9 1.0 collective-permute-start
  45.9 6.3 %collective-permute-done = bf16[8,128,128]{1,0,2:T(8,128)(2,1)S(1)} collective-permute-done((bf16[8,128,128]{1,0,2:T(8,128)(2,1)S(1)}, bf16[8,128,128]{1,0,2:T(8,128)(2,1)S(1)}, u32[]{:S(2)}, u32[]{:S(2)}) %collective-permute-start) | collective-permute-done | bytes 262176 | tf_op jit(solution)/shard_map/ppermute | solution.py:62
  52.3 0.7 fusion.6
  53.0 7.0 %collective-permute-done.1 = bf16[8,128,128]{1,0,2:T(8,128)(2,1)S(1)} collective-permute-done((bf16[8,128,128]{1,0,2:T(8,128)(2,1)S(1)}, bf16[8,128,128]{1,0,2:T(8,128)(2,1)S(1)}, u32[]{:S(2)}, u32[]{:S(2)}) %collective-permute-start.1) | collective-permute-done | bytes 262176 | tf_op jit(solution)/shard_map/ppermute | solution.py:62
  60.0 1.9 %copy.94 = bf16[32,128,128]{1,0,2:T(8,128)(2,1)S(1)} copy(bf16[32,128,128]{2,1,0:T(8,128)(2,1)} %all-gather.4.cloned.1.call-done) | data formatting | bytes 2097152 | tf_op jit(solution)/shard_map/all_gather | solution.py:56
  61.9 0.6 convolution_bitcast_fusion.3
  62.8 0.6 convolution_bitcast_fusion.2
  63.7 0.6 convolution_bitcast_fusion.1
  64.6 2.8 %collective-permute-done.2 = bf16[8,128,128]{1,0,2:T(8,128)(2,1)} collective-permute-done((bf16[8,128,128]{1,0,2:T(8,128)(2,1)S(1)}, bf16[8,128,128]{1,0,2:T(8,128)(2,1)}, u32[]{:S(2)}, u32[]{:S(2)}) %collective-permute-start.2) | collective-permute-done | bytes 262176 | tf_op jit(solution)/shard_map/ppermute | solution.py:62
  67.4 1.6 %convolution_bitcast_fusion = f32[32,8,128]{0,1,2:T(8,128)S(1)} fusion(bf16[8,128,128]{1,0,2:T(8,128)(2,1)} %collective-permute-done.2, bf16[32,128,128]{1,0,2:T(8,128)(2,1)S(1)} %copy.94), kind=kOutput, calls=%fused_computation.13 | convolution fusion | flops 8388608 | bytes 1441792 | tf_op jit(solution)/shard_map/ikh,jkh->ijh/dot_general | solution.py:63
  70.0 0.8 fusion.62
  72.2 1.0 fusion.20
  73.4 10.8 %all_to_all.48 = bf16[32,32,128]{2,0,1:T(8,128)(2,1)S(1)} all-to-all(bf16[32,32,128]{2,0,1:T(8,128)(2,1)S(1)} %copy.103), channel_id=1, replica_groups=mesh['row'=4,'col'=4,'crop'=2] {'col'}, dimensions={1} | all-to-all | bytes 524288 | tf_op jit(solution)/shard_map/all_to_all | solution.py:73
  84.2 8.1 %all_to_all.49 = bf16[32,32,128]{2,0,1:T(8,128)(2,1)S(1)} all-to-all(bf16[32,32,128]{2,0,1:T(8,128)(2,1)S(1)} %all_to_all.48), channel_id=1, replica_groups=mesh['row'=4,'col'=4,'crop'=2] {'row'}, dimensions={1} | all-to-all | bytes 524288 | tf_op jit(solution)/shard_map/all_to_all | solution.py:72
  92.5 0.9 copy.106
  93.4 1.1 fusion.3
  94.5 3.8 %all-gather.6.cloned.1.call-done = bf16[128,32,128]{2,1,0:T(8,128)(2,1)} async-done(((bf16[32,32,128]{2,1,0:T(8,128)(2,1)}), bf16[128,32,128]{2,1,0:T(8,128)(2,1)}) %all-gather.6.cloned.1.call-update) | async-done | bytes 1048592 | tf_op jit(solution)/shard_map/all_gather | solution.py:80
  98.3 3.2 %copy.107 = bf16[128,32,128]{0,1,2:T(8,128)(2,1)} copy(bf16[128,32,128]{2,1,0:T(8,128)(2,1)} %all-gather.6.cloned.1.call-done) | data formatting | bytes 2097152 | tf_op jit(solution)/shard_map/all_gather | solution.py:80
  101.5 28.3 %all-gather.8.cloned.1.call-done = bf16[128,32,128]{0,1,2:T(8,128)(2,1)} async-done(((bf16[128,8,128]{0,1,2:T(8,128)(2,1)}), bf16[128,32,128]{0,1,2:T(8,128)(2,1)}) %all-gather.8.cloned.1.call-update) | async-done | bytes 1048592 | tf_op jit(solution)/shard_map/all_gather | solution.py:83
  129.9 2.2 %bitcast_reduce_fusion = (f32[32,32]{0,1:T(8,128)S(1)}, f32[128,32,32]{2,1,0:T(8,128)S(1)}) fusion(bf16[128,32,128]{0,1,2:T(8,128)(2,1)} %copy.107, bf16[128,32,128]{0,1,2:T(8,128)(2,1)} %all-gather.8.cloned.1.call-done), kind=kOutput, calls=%fused_computation.3 | convolution fusion | flops 33684480 | bytes 2625536 | tf_op jit(solution)/shard_map/kih,kjh->ijh/dot_general | solution.py:81
  132.8 1.3 multiply_convert_fusion
  134.0 2.6 %copy.112 = bf16[32,32,128]{2,1,0:T(8,128)(2,1)S(1)} copy(bf16[32,32,128]{0,1,2:T(8,128)(2,1)} %multiply_convert_fusion) | data formatting | bytes 524288 | tf_op jit(solution)/shard_map/convert_element_type | solution.py:26
  136.7 1.4 fusion.63
  138.5 0.8 fusion.39
  139.4 1.4 fusion.13
  (65 shorter events, 4.8 us)
Async XLA Ops:
  6.5 131.9 %copy-start = (bf16[128,1024]{1,0:T(8,128)(2,1)S(1)}, bf16[128,1024]{1,0:T(8,128)(2,1)}, u32[]{:S(2)}) copy-start(bf16[128,1024]{1,0:T(8,128)(2,1)} %param.22) | copy-start | bytes 786436
  6.5 4.0 %copy-start.1 = (bf16[32,32,128]{2,1,0:T(8,128)(2,1)S(1)}, bf16[32,32,128]{2,1,0:T(8,128)(2,1)}, u32[]{:S(2)}) copy-start(bf16[32,32,128]{2,1,0:T(8,128)(2,1)} %param.12) | copy-start | bytes 786436
  6.5 5.3 %copy-start.6 = (s32[32,32]{1,0:T(8,128)S(1)}, s32[32,32]{1,0:T(8,128)}, u32[]{:S(2)}) copy-start(s32[32,32]{1,0:T(8,128)} %param.13) | copy-start | bytes 12292
  6.5 53.5 %all-gather.4.cloned.1.call-start = ((), (), s32[]{:S(2)}) async-start(), calls=%async_computation.4 | async-start | bytes 1310720 | tf_op jit(solution)/shard_map/all_gather | solution.py:56
  11.9 40.5 %copy-start.8 = (bf16[128,128]{1,0:T(8,128)(2,1)S(1)}, bf16[128,128]{1,0:T(8,128)(2,1)}, u32[]{:S(2)}) copy-start(bf16[128,128]{1,0:T(8,128)(2,1)} %param.16) | copy-start | bytes 98308
  12.9 85.4 %all-gather.6.cloned.1.call-start = ((), (), s32[]{:S(2)}) async-start(), calls=%async_computation.5 | async-start | bytes 1310720 | tf_op jit(solution)/shard_map/all_gather | solution.py:80
  44.9 7.3 %collective-permute-start = (bf16[8,128,128]{1,0,2:T(8,128)(2,1)S(1)}, bf16[8,128,128]{1,0,2:T(8,128)(2,1)S(1)}, u32[]{:S(2)}, u32[]{:S(2)}) collective-permute-start(bf16[8,128,128]{1,0,2:T(8,128)(2,1)S(1)} %copy.93), channel_id=1, source_target_pairs={{0,8},{8,16},{16,24},{24,0},{1,9},{9,17},{17,25},{25,1},{2,10},{10... | collective-permute-start | bytes 786440 | tf_op jit(solution)/shard_map/ppermute | solution.py:62
  52.2 7.8 %collective-permute-start.1 = (bf16[8,128,128]{1,0,2:T(8,128)(2,1)S(1)}, bf16[8,128,128]{1,0,2:T(8,128)(2,1)S(1)}, u32[]{:S(2)}, u32[]{:S(2)}) collective-permute-start(bf16[8,128,128]{1,0,2:T(8,128)(2,1)S(1)} %collective-permute-done), channel_id=1, source_target_pairs={{0,8},{8,16},{16,24},{24,0},{1,9},{9,17},{17,25},{25,1},{2,10},{10... | collective-permute-start | bytes 786440 | tf_op jit(solution)/shard_map/ppermute | solution.py:62
  60.0 7.4 %collective-permute-start.2 = (bf16[8,128,128]{1,0,2:T(8,128)(2,1)S(1)}, bf16[8,128,128]{1,0,2:T(8,128)(2,1)}, u32[]{:S(2)}, u32[]{:S(2)}) collective-permute-start(bf16[8,128,128]{1,0,2:T(8,128)(2,1)S(1)} %collective-permute-done.1), channel_id=1, source_target_pairs={{0,8},{8,16},{16,24},{24,0},{1,9},{9,17},{17,25},{25,1},{2,10},{10... | collective-permute-start | bytes 786440 | tf_op jit(solution)/shard_map/ppermute | solution.py:62
  69.0 1.0 copy-start.5
  69.6 2.0 %copy-start.2 = (bf16[128,256]{1,0:T(8,128)(2,1)S(1)}, bf16[128,256]{1,0:T(8,128)(2,1)}, u32[]{:S(2)}) copy-start(bf16[128,256]{1,0:T(8,128)(2,1)} %param.18) | copy-start | bytes 196612
  70.0 1.9 %copy-start.3 = (bf16[128,256]{1,0:T(8,128)(2,1)S(1)}, bf16[128,256]{1,0:T(8,128)(2,1)}, u32[]{:S(2)}) copy-start(bf16[128,256]{1,0:T(8,128)(2,1)} %param.19) | copy-start | bytes 196612
  73.2 20.2 %copy-start.9 = (bf16[128,128]{1,0:T(8,128)(2,1)S(1)}, bf16[128,128]{1,0:T(8,128)(2,1)}, u32[]{:S(2)}) copy-start(bf16[128,128]{1,0:T(8,128)(2,1)} %param.20) | copy-start | bytes 98308
  73.2 56.6 %all-gather.8.cloned.1.call-start = ((), (), s32[]{:S(2)}) async-start(), calls=%async_computation.6 | async-start | bytes 1310720 | tf_op jit(solution)/shard_map/all_gather | solution.py:83
  132.8 3.9 %copy-start.4 = (bf16[128,128]{1,0:T(8,128)(2,1)S(1)}, bf16[128,128]{1,0:T(8,128)(2,1)}, u32[]{:S(2)}) copy-start(bf16[128,128]{1,0:T(8,128)(2,1)} %param.21) | copy-start | bytes 98308
  138.5 0.9 copy-start.7
Sparse Core Ops, SparseCore 0:
  13.1 36.7 all-gather.3
  73.4 24.9 all-gather.5
  99.9 29.9 all-gather.7
